TPU v7x, 32 devices: a whole 2x2x4 slice. The times are simulated.
32 devices in a mesh: row: 8 (over y, x, core), col: 4 (over z).
Axes of the slice: x: 2, y: 2, z: 4, core: 2. Of those that a mesh axis runs over, the one named last changes fastest.
Arguments:
- vectors: bfloat16 [32, 1024, 512], P('col', 'row'), may hold values from -6 to 6
- right_factors: bfloat16 [32, 32, 1024, 128], P('row', 'col'), may hold values from -0.1875 to 0.1875
- left_factors: bfloat16 [32, 32, 1024, 128], P('row', 'col'), may hold values from -0.125 to 0.125
- tile_ranks: int32 [32, 32], P('row', 'col'), may hold values from 16 to 128
- owner_map: int32 [32], replicated, may hold values from 0 to 31, as said below
Outputs:
- applied: bfloat16 [32, 1024, 512], P('row', 'col')
Inputs may be any that keep to these rules, and one draw needn't show every extreme that they name: owner_map is a permutation of 0 to 31; the 4 stored tile rows held by index i of row (stored rows i * 4 to i * 4 + 3) belong to 4 different indices of row of applied, i + c mod 8 for the same 4 offsets c at every i.
All inputs are finite; a program needn't handle non-finite values.
Results may differ from a plain program's by a relative error of at most 0.0066.
Values may be sent and summed in bfloat16 or wider, within the bound.
A program may use at most 128 MiB of HBM per device.

v0:
```python
import jax
import jax.numpy as jnp
from jax import lax
from jax.sharding import PartitionSpec as P


def masked_coeffs(products, tile_ranks, rank_width):
    columns = jnp.arange(rank_width, dtype=jnp.int32)
    kept_mask = columns[None, None, :] < tile_ranks[:, :, None]
    return jnp.where(kept_mask[:, :, :, None], products, 0.0).astype(jnp.bfloat16)


def build_buffer(payload, owner_map, cycle_size):
    held_rows = payload.shape[0]
    own_rows = lax.dynamic_slice_in_dim(owner_map, lax.axis_index("row") * held_rows, held_rows)
    target = own_rows // held_rows
    devices = jnp.arange(cycle_size, dtype=jnp.int32)
    matches = target[None, :] == devices[:, None]
    present = jnp.any(matches, axis=1)
    source_slot = jnp.sum(
        jnp.where(matches, jnp.arange(held_rows, dtype=jnp.int32)[None, :], 0), axis=1
    )
    picked = jnp.take(payload, source_slot, axis=0)
    return jnp.where(present[:, None, None], picked, jnp.zeros_like(picked))


def pick_rows(received, owner_map, held_rows):
    wanted = lax.axis_index("row") * held_rows + jnp.arange(held_rows, dtype=jnp.int32)
    matches = owner_map[None, :] == wanted[:, None]
    anchor = jnp.sum(
        jnp.where(matches, jnp.arange(owner_map.shape[0], dtype=jnp.int32)[None, :], 0), axis=1
    )
    return jnp.take(received, anchor // held_rows, axis=0)


def on_device(vectors, right_factors, left_factors, tile_ranks, owner_map):
    held_rows = right_factors.shape[0]
    rank_width = right_factors.shape[3]
    cycle_size = lax.axis_size("row")
    products = jnp.einsum(
        "ikbr,kbv->ikrv",
        right_factors,
        lax.all_gather(vectors, "row", axis=1, tiled=True),
        preferred_element_type=jnp.float32,
    )
    coeffs = masked_coeffs(products, tile_ranks, rank_width)
    partial_rows = jnp.einsum(
        "ikbr,ikrv->ibv", left_factors, coeffs, preferred_element_type=jnp.float32
    )
    summed = lax.psum_scatter(partial_rows, "col", scatter_dimension=1, tiled=True).astype(
        jnp.bfloat16
    )
    buffer = build_buffer(summed, owner_map, cycle_size)
    received = lax.all_to_all(buffer, "row", split_axis=0, concat_axis=0, tiled=True)
    applied = pick_rows(received, owner_map, held_rows)
    return applied


def solution(mesh):
    placed = (
        P("col", "row", None),
        P("row", "col", None, None),
        P("row", "col", None, None),
        P("row", "col"),
        P(),
    )
    return jax.shard_map(
        on_device, mesh=mesh, in_specs=placed, out_specs=P("row", "col", None), check_vma=False
    )
```

profile of v0, /device:TPU:0, one launch (start us, length us, event | category | flops | bytes accessed | tf_op | source)
XLA Modules:
  0.0 271.4 jit_solution(948302696471374495)
XLA Ops:
  6.5 0.0 all-gather.2.cloned.1.call-start
  6.5 0.7 all-gather.2.cloned.1.call-update
  7.3 0.0 reduce-scatter.2.cloned.1.call-start
  7.3 0.8 iota_compare_fusion
  8.1 58.2 %all-gather.2.cloned.1.call-done = bf16[8,1024,512]{2,1,0:T(8,128)(2,1)} async-done(((bf16[8,128,512]{2,1,0:T(8,128)(2,1)}), bf16[8,1024,512]{2,1,0:T(8,128)(2,1)}) %all-gather.2.cloned.1.call-update) | async-done | bytes 8388624 | tf_op jit(solution)/shard_map/all_gather | solution.py:43
  66.3 17.0 %fusion.7 = f32[4,1024,512]{1,2,0:T(8,128)} fusion(bf16[4,8,1024,128]{3,2,1,0:T(8,128)(2,1)} %param.7, pred[4,8,128]{2,1,0:T(8,128)(4,1)S(1)} %iota_compare_fusion, bf16[4,8,1024,128]{3,2,1,0:T(8,128)(2,1)} %param.6, bf16[8,1024,512]{2,1,0:T(8,128)(2,1)} %all-gather.2.cloned.1.call-done), kind=kOutput, calls=%fused_computation.9 | convolution fusion | flops 8594128896 | bytes 33558528 | tf_op jit(solution)/shard_map/ikbr,ikrv->ibv/dot_general | solution.py:47
  83.3 0.0 copy-start
  83.3 0.0 reduce-scatter.2.cloned.1.call-update
  83.3 0.6 copy-done
  83.9 0.1 and_select_fusion.1
  84.0 0.1 select_reduce_fusion
  84.1 0.1 fusion.14
  84.2 143.9 %reduce-scatter.2.cloned.1.call-done = f32[4,256,512]{1,2,0:T(8,128)} async-done(((f32[4,1024,512]{1,2,0:T(8,128)}), f32[4,256,512]{1,2,0:T(8,128)}) %reduce-scatter.2.cloned.1.call-update) | async-done | bytes 2097168 | tf_op jit(solution)/shard_map/reduce_scatter | solution.py:50
  228.1 1.7 convert_element_type.7
  229.8 0.7 gather_fusion
  230.5 1.6 select_select_fusion
  232.1 3.7 %all-to-all-start = ((bf16[8,256,512]{1,2,0:T(8,128)(2,1)}), bf16[8,256,512]{1,2,0:T(8,128)(2,1)S(1)}, u32[]{:S(2)}, u32[]{:S(2)}) async-start(bf16[8,256,512]{1,2,0:T(8,128)(2,1)} %select_select_fusion), calls=%async_computation.1 | async-start | bytes 4194304 | tf_op jit(solution)/shard_map/all_to_all | solution.py:54
  235.8 0.2 select_reduce_fusion.1
  236.0 26.4 %all-to-all-done = bf16[8,256,512]{1,2,0:T(8,128)(2,1)S(1)} async-done(((bf16[8,256,512]{1,2,0:T(8,128)(2,1)}), bf16[8,256,512]{1,2,0:T(8,128)(2,1)S(1)}, u32[]{:S(2)}, u32[]{:S(2)}) %all-to-all-start) | async-done | bytes 2097184 | tf_op jit(solution)/shard_map/all_to_all | solution.py:54
  262.4 0.6 gather_fusion.1
  263.0 0.2 broadcast_select_fusion
  263.2 1.3 copy.7
  (7 shorter events, 0.1 us)
Async XLA Ops:
  6.5 59.7 %all-gather.2.cloned.1.call-start = ((), (), s32[]{:S(2)}) async-start(), calls=%async_computation.2 | async-start | bytes 9437184 | tf_op jit(solution)/shard_map/all_gather | solution.py:43
  7.3 220.8 %reduce-scatter.2.cloned.1.call-start = ((), (), s32[]{:S(2)}) async-start(), calls=%async_computation.3 | async-start | bytes 10485760 | tf_op jit(solution)/shard_map/reduce_scatter | solution.py:50
  83.3 0.7 copy-start
  232.1 30.3 %all-to-all-start = ((bf16[8,256,512]{1,2,0:T(8,128)(2,1)}), bf16[8,256,512]{1,2,0:T(8,128)(2,1)S(1)}, u32[]{:S(2)}, u32[]{:S(2)}) async-start(bf16[8,256,512]{1,2,0:T(8,128)(2,1)} %select_select_fusion), calls=%async_computation.1 | async-start | bytes 4194304 | tf_op jit(solution)/shard_map/all_to_all | solution.py:54
Sparse Core Ops, SparseCore 0:
  9.2 56.9 all-gather.1
  83.4 144.6 reduce-scatter.1
where the time goes:
time: 272 us; the launch traced here: 271 us
  waiting for transfers between devices  229 us (84%)
  matrix products  17 us (6%)
  between operations  13.4 us (5%)
  other arithmetic  4.76 us (2%)
  starting transfers between devices  3.7 us (1%)
  local copies, waits for them, and re-layouts  3.24 us (1%)
    reduce_scatter x1, waiting for transfers between devices, on_device(): lax.psum_scatter(partial_rows, 'col', scatter_dimension=1, tiled=True)  144 us
    all_gather x1, waiting for transfers between devices, on_device(): lax.all_gather(vectors, 'row', axis=1, tiled=True)  58.2 us
    all_to_all x1, waiting for transfers between devices, on_device(): lax.all_to_all(buffer, 'row', split_axis=0, concat_axis=0, tiled=True)  26.4 us
    dot_general x1, matrix products, on_device(): jnp.einsum('ikbr,ikrv->ibv', left_factors, coeffs, preferred_element_type...  17 us
  transfers between devices with their start and end apart: 3, of which 3 were waited for; matrix products, arithmetic and copies ran while one was open for 0% of the time, Pallas kernels for 0%

commit v1 on v0

--- a/solution.py
+++ b/solution.py
@@ -37,11 +37,35 @@
     held_rows = right_factors.shape[0]
     rank_width = right_factors.shape[3]
     cycle_size = lax.axis_size("row")
-    products = jnp.einsum(
-        "ikbr,kbv->ikrv",
-        right_factors,
-        lax.all_gather(vectors, "row", axis=1, tiled=True),
-        preferred_element_type=jnp.float32,
+
+    def answer_spot_in(patch, dim_no, block_here):
+        small = lax.axis_size("row")
+        e_now, tall, shaped = (small, lax.axis_index("row"), patch.shape[dim_no])
+        arrivals = list(map(lambda k: (k, (k + 1) % e_now), range(e_now)))
+        gallery = list(map(lambda k: (k, (k - 1) % e_now), range(e_now)))
+        carry_in = e_now // 2
+        raw_out = clean = patch
+        frame_out = block_here(patch, tall * shaped)
+        m = 1
+        while m < carry_in + 1:
+            raw_out = lax.ppermute(raw_out, "row", arrivals)
+            if m < e_now - carry_in:
+                clean = lax.ppermute(clean, "row", gallery)
+                frame_out = frame_out + block_here(clean, (tall + m) % e_now * shaped)
+            item_now = block_here(raw_out, (tall - m) % e_now * shaped)
+            frame_out = frame_out + item_now
+            m = m + 1
+        return frame_out
+
+    products = answer_spot_in(
+        vectors,
+        dim_no=1,
+        block_here=lambda own_block, offset: jnp.einsum(
+            "ikbr,kbv->ikrv",
+            lax.dynamic_slice_in_dim(right_factors, offset, own_block.shape[1], axis=2),
+            own_block,
+            preferred_element_type=jnp.float32,
+        ),
     )
     coeffs = masked_coeffs(products, tile_ranks, rank_width)
     partial_rows = jnp.einsum(

time: 272 us -> 309 us (1.14)
  matrix products: 17 us -> 59.6 us
  waiting for transfers between devices: 229 us -> 213 us
  starting transfers between devices: 3.7 us -> 15 us
    all_gather x1 -> x0, waiting for transfers between devices: 58.2 us -> none  [on_device(): lax.all_gather(vectors, 'row', axis=1, tiled=True)]
    ppermute x0 -> x7, waiting for transfers between devices: none -> 40.1 us  [the longest x4 36.6 us: answer_spot_in(): raw_out = lax.ppermute(raw_out, 'row', arrivals)]
    dot_general x0 -> x7, matrix products: none -> 33.2 us  [on_device(): jnp.einsum('ikbr,kbv->ikrv', lax.dynamic_slice_in_dim(right_factors, offs...]
    ppermute x0 -> x7, starting transfers between devices: none -> 11.4 us  [the longest x3 7.61 us: answer_spot_in(): clean = lax.ppermute(clean, 'row', gallery)]
    dot_general x1, matrix products: 17 us -> 26.4 us  [on_device(): jnp.einsum('ikbr,ikrv->ibv', left_factors, coeffs, preferred_element_type...]
  transfers between devices with their start and end apart: 3 -> 9, of which waited for: 3 -> 8; matrix products, arithmetic and copies ran while one was open for 0% -> 11% of each run, Pallas kernels for 0% -> 0%
where the time goes in v1:
time: 309 us
  waiting for transfers between devices  213 us (69%)
  matrix products  59.6 us (19%)
  starting transfers between devices  15 us (5%)
  between operations  13.4 us (4%)
  other arithmetic  4.06 us (1%)
  local copies, waits for them, and re-layouts  3.25 us (1%)
    reduce_scatter x1, waiting for transfers between devices, on_device(): lax.psum_scatter(partial_rows, 'col', scatter_dimension=1, tiled=True)  147 us
    ppermute x4, waiting for transfers between devices, answer_spot_in(): raw_out = lax.ppermute(raw_out, 'row', arrivals)  36.6 us
    dot_general x7, matrix products, on_device(): jnp.einsum('ikbr,kbv->ikrv', lax.dynamic_slice_in_dim(right_factors, offs...  33.2 us
    all_to_all x1, waiting for transfers between devices, on_device(): lax.all_to_all(buffer, 'row', split_axis=0, concat_axis=0, tiled=True)  26.4 us
    dot_general x1, matrix products, on_device(): jnp.einsum('ikbr,ikrv->ibv', left_factors, coeffs, preferred_element_type...  26.4 us
    ppermute x3, starting transfers between devices, answer_spot_in(): clean = lax.ppermute(clean, 'row', gallery)  7.61 us
  transfers between devices with their start and end apart: 9, of which 8 were waited for; matrix products, arithmetic and copies ran while one was open for 11% of the time, Pallas kernels for 0%

profile of v1, /device:TPU:0, one launch (start us, length us, event | category | flops | bytes accessed | tf_op | source)
XLA Modules:
  0.0 308.6 jit_solution(6477970531412108000)
XLA Ops:
  6.5 0.0 copy-start.1
  6.5 0.0 reduce-scatter.2.cloned.1.call-start
  6.5 0.5 collective-permute-start.1
  7.0 2.9 collective-permute-start
  9.9 21.3 %collective-permute-done.1 = bf16[8,128,512]{2,1,0:T(8,128)(2,1)S(1)} collective-permute-done((bf16[8,128,512]{2,1,0:T(8,128)(2,1)}, bf16[8,128,512]{2,1,0:T(8,128)(2,1)S(1)}, u32[]{:S(2)}, u32[]{:S(2)}) %collective-permute-start.1) | collective-permute-done | bytes 1048608 | tf_op jit(solution)/shard_map/ppermute | solution.py:51
  31.2 0.7 collective-permute-start.3
  31.9 0.0 copy-start
  31.9 6.2 %fusion.24 = f32[8,4,128,512]{2,3,0,1:T(8,128)} fusion(bf16[8,128,512]{2,1,0:T(8,128)(2,1)} %param.5, bf16[4,8,1024,128]{3,2,1,0:T(8,128)(2,1)} %param.6, s32[]{:T(128)S(6)} %select_n.139), kind=kOutput, calls=%fused_computation.23 | convolution fusion | flops 536870912 | bytes 10485764 | tf_op jit(solution)/shard_map/ikbr,kbv->ikrv/dot_general | solution.py:63
  38.2 0.0 collective-permute-done
  38.2 1.9 collective-permute-start.2
  40.1 0.0 copy-done.1
  40.1 0.1 iota_compare_fusion
  40.2 8.6 %collective-permute-done.3 = bf16[8,128,512]{2,1,0:T(8,128)(2,1)S(1)} collective-permute-done((bf16[8,128,512]{2,1,0:T(8,128)(2,1)S(1)}, bf16[8,128,512]{2,1,0:T(8,128)(2,1)S(1)}, u32[]{:S(2)}, u32[]{:S(2)}) %collective-permute-start.3) | collective-permute-done | bytes 1048608 | tf_op jit(solution)/shard_map/ppermute | solution.py:51
  48.8 2.0 collective-permute-start.5
  50.8 0.0 copy-done
  50.8 4.5 %fusion.20 = f32[8,4,128,512]{2,3,0,1:T(8,128)} fusion(bf16[8,128,512]{2,1,0:T(8,128)(2,1)S(1)} %collective-permute-done.1, bf16[4,8,1024,128]{3,2,1,0:T(8,128)(2,1)S(1)} %copy-done, s32[]{:T(128)S(6)} %select_n.143), kind=kOutput, calls=%fused_computation.19 | convolution fusion | flops 536870912 | bytes 10485764 | tf_op jit(solution)/shard_map/ikbr,kbv->ikrv/dot_general | solution.py:63
  55.3 4.5 %fusion.22 = f32[8,4,128,512]{2,3,0,1:T(8,128)} fusion(bf16[8,128,512]{2,1,0:T(8,128)(2,1)S(1)} %collective-permute-done, bf16[4,8,1024,128]{3,2,1,0:T(8,128)(2,1)S(1)} %copy-done, s32[]{:T(128)S(6)} %select_n.141), kind=kOutput, calls=%fused_computation.21 | convolution fusion | flops 536870912 | bytes 10485764 | tf_op jit(solution)/shard_map/ikbr,kbv->ikrv/dot_general | solution.py:63
  59.8 0.8 collective-permute-done.2
  60.7 2.8 collective-permute-start.4
  63.5 4.5 %fusion.16 = f32[8,4,128,512]{2,3,0,1:T(8,128)} fusion(bf16[8,128,512]{2,1,0:T(8,128)(2,1)S(1)} %collective-permute-done.3, bf16[4,8,1024,128]{3,2,1,0:T(8,128)(2,1)S(1)} %copy-done, s32[]{:T(128)S(6)} %select_n.147), kind=kOutput, calls=%fused_computation.15 | convolution fusion | flops 536870912 | bytes 10485764 | tf_op jit(solution)/shard_map/ikbr,kbv->ikrv/dot_general | solution.py:63
  68.0 3.9 %collective-permute-done.5 = bf16[8,128,512]{2,1,0:T(8,128)(2,1)S(1)} collective-permute-done((bf16[8,128,512]{2,1,0:T(8,128)(2,1)S(1)}, bf16[8,128,512]{2,1,0:T(8,128)(2,1)S(1)}, u32[]{:S(2)}, u32[]{:S(2)}) %collective-permute-start.5) | collective-permute-done | bytes 1048608 | tf_op jit(solution)/shard_map/ppermute | solution.py:51
  71.9 0.5 collective-permute-start.6
  72.4 4.5 %fusion.18 = f32[8,4,128,512]{2,3,0,1:T(8,128)} fusion(bf16[8,128,512]{2,1,0:T(8,128)(2,1)S(1)} %collective-permute-done.2, bf16[4,8,1024,128]{3,2,1,0:T(8,128)(2,1)S(1)} %copy-done, s32[]{:T(128)S(6)} %select_n.145), kind=kOutput, calls=%fused_computation.17 | convolution fusion | flops 536870912 | bytes 10485764 | tf_op jit(solution)/shard_map/ikbr,kbv->ikrv/dot_general | solution.py:63
  76.9 4.5 %fusion.12 = f32[8,4,128,512]{2,3,0,1:T(8,128)} fusion(bf16[8,128,512]{2,1,0:T(8,128)(2,1)S(1)} %collective-permute-done.5, bf16[4,8,1024,128]{3,2,1,0:T(8,128)(2,1)S(1)} %copy-done, s32[]{:T(128)S(6)} %select_n.151), kind=kOutput, calls=%fused_computation.11 | convolution fusion | flops 536870912 | bytes 10485764 | tf_op jit(solution)/shard_map/ikbr,kbv->ikrv/dot_general | solution.py:63
  81.4 2.6 collective-permute-done.4
  84.0 4.5 %fusion.14 = f32[8,4,128,512]{2,3,0,1:T(8,128)} fusion(bf16[8,128,512]{2,1,0:T(8,128)(2,1)S(1)} %collective-permute-done.4, bf16[4,8,1024,128]{3,2,1,0:T(8,128)(2,1)S(1)} %copy-done, s32[]{:T(128)S(6)} %select_n.149), kind=kOutput, calls=%fused_computation.13 | convolution fusion | flops 536870912 | bytes 10485764 | tf_op jit(solution)/shard_map/ikbr,kbv->ikrv/dot_general | solution.py:63
  88.5 2.8 collective-permute-done.6
  91.3 26.4 %fusion.5 = f32[4,1024,512]{1,2,0:T(8,128)} fusion(bf16[4,8,1024,128]{3,2,1,0:T(8,128)(2,1)} %param.7, f32[8,4,128,512]{2,3,0,1:T(8,128)} %fusion.12, f32[8,4,128,512]{2,3,0,1:T(8,128)} %fusion.14, f32[8,4,128,512]{2,3,0,1:T(8,128)} %fusion.16, f32[8,4,128,512]{2,3,0,1:T(8,128)} %fusion.18, f32[8,4,128,512]{2,3,0,1:T(8,128)} %fusion.20, ...), kind=kOutput, calls=%fused_computation.7 | convolution fusion | flops 4850712576 | bytes 77598720 | tf_op jit(solution)/shard_map/ikbr,ikrv->ibv/dot_general | solution.py:71
  117.7 0.0 copy-start.2
  117.7 0.0 reduce-scatter.2.cloned.1.call-update
  117.7 0.6 copy-done.2
  118.3 0.1 and_select_fusion.1
  118.4 0.1 select_reduce_fusion
  118.5 0.1 fusion.35
  118.6 146.7 %reduce-scatter.2.cloned.1.call-done = f32[4,256,512]{1,2,0:T(8,128)} async-done(((f32[4,1024,512]{1,2,0:T(8,128)}), f32[4,256,512]{1,2,0:T(8,128)}) %reduce-scatter.2.cloned.1.call-update) | async-done | bytes 2097168 | tf_op jit(solution)/shard_map/reduce_scatter | solution.py:74
  265.4 1.7 convert_element_type.7
  267.0 0.7 gather_fusion
  267.7 1.6 select_select_fusion
  269.4 3.7 %all-to-all-start = ((bf16[8,256,512]{1,2,0:T(8,128)(2,1)}), bf16[8,256,512]{1,2,0:T(8,128)(2,1)S(1)}, u32[]{:S(2)}, u32[]{:S(2)}) async-start(bf16[8,256,512]{1,2,0:T(8,128)(2,1)} %select_select_fusion), calls=%async_computation.1 | async-start | bytes 4194304 | tf_op jit(solution)/shard_map/all_to_all | solution.py:78
  273.0 0.2 select_reduce_fusion.1
  273.3 26.4 %all-to-all-done = bf16[8,256,512]{1,2,0:T(8,128)(2,1)S(1)} async-done(((bf16[8,256,512]{1,2,0:T(8,128)(2,1)}), bf16[8,256,512]{1,2,0:T(8,128)(2,1)S(1)}, u32[]{:S(2)}, u32[]{:S(2)}) %all-to-all-start) | async-done | bytes 2097184 | tf_op jit(solution)/shard_map/all_to_all | solution.py:78
  299.6 0.6 gather_fusion.1
  300.3 0.2 broadcast_select_fusion
  300.4 1.3 copy.7
  (7 shorter events, 0.1 us)
Async XLA Ops:
  6.5 33.6 %copy-start.1 = (s32[4,8]{1,0:T(4,128)S(1)}, s32[4,8]{1,0:T(4,128)}, u32[]{:S(2)}) copy-start(s32[4,8]{1,0:T(4,128)} %param.8) | copy-start | bytes 388
  6.5 258.8 %reduce-scatter.2.cloned.1.call-start = ((), (), s32[]{:S(2)}) async-start(), calls=%async_computation.2 | async-start | bytes 10485760 | tf_op jit(solution)/shard_map/reduce_scatter | solution.py:74
  6.5 24.7 %collective-permute-start.1 = (bf16[8,128,512]{2,1,0:T(8,128)(2,1)}, bf16[8,128,512]{2,1,0:T(8,128)(2,1)S(1)}, u32[]{:S(2)}, u32[]{:S(2)}) collective-permute-start(bf16[8,128,512]{2,1,0:T(8,128)(2,1)} %param.5), channel_id=1, source_target_pairs={{0,4},{4,8},{8,12},{12,16},{16,20},{20,24},{24,28},{28,0},{1,5},{5... | collective-permute-start | bytes 3145736 | tf_op jit(solution)/shard_map/ppermute | solution.py:51
  7.0 31.1 %collective-permute-start = (bf16[8,128,512]{2,1,0:T(8,128)(2,1)}, bf16[8,128,512]{2,1,0:T(8,128)(2,1)S(1)}, u32[]{:S(2)}, u32[]{:S(2)}) collective-permute-start(bf16[8,128,512]{2,1,0:T(8,128)(2,1)} %param.5), channel_id=1, source_target_pairs={{0,28},{4,0},{8,4},{12,8},{16,12},{20,16},{24,20},{28,24},{1,29},{... | collective-permute-start | bytes 3145736 | tf_op jit(solution)/shard_map/ppermute | solution.py:53
  31.2 17.6 %collective-permute-start.3 = (bf16[8,128,512]{2,1,0:T(8,128)(2,1)S(1)}, bf16[8,128,512]{2,1,0:T(8,128)(2,1)S(1)}, u32[]{:S(2)}, u32[]{:S(2)}) collective-permute-start(bf16[8,128,512]{2,1,0:T(8,128)(2,1)S(1)} %collective-permute-done.1), channel_id=1, source_target_pairs={{0,4},{4,8},{8,12},{12,16},{16,20},{20,24},{24,28},{28,0},{1,5},{5... | collective-permute-start | bytes 3145736 | tf_op jit(solution)/shard_map/ppermute | solution.py:51
  31.9 18.9 %copy-start = (bf16[4,8,1024,128]{3,2,1,0:T(8,128)(2,1)S(1)}, bf16[4,8,1024,128]{3,2,1,0:T(8,128)(2,1)}, u32[]{:S(2)}) copy-start(bf16[4,8,1024,128]{3,2,1,0:T(8,128)(2,1)} %param.6) | copy-start | bytes 25165828
  38.2 22.5 %collective-permute-start.2 = (bf16[8,128,512]{2,1,0:T(8,128)(2,1)S(1)}, bf16[8,128,512]{2,1,0:T(8,128)(2,1)S(1)}, u32[]{:S(2)}, u32[]{:S(2)}) collective-permute-start(bf16[8,128,512]{2,1,0:T(8,128)(2,1)S(1)} %collective-permute-done), channel_id=1, source_target_pairs={{0,28},{4,0},{8,4},{12,8},{16,12},{20,16},{24,20},{28,24},{1,29},{... | collective-permute-start | bytes 3145736 | tf_op jit(solution)/shard_map/ppermute | solution.py:53
  48.8 23.1 %collective-permute-start.5 = (bf16[8,128,512]{2,1,0:T(8,128)(2,1)S(1)}, bf16[8,128,512]{2,1,0:T(8,128)(2,1)S(1)}, u32[]{:S(2)}, u32[]{:S(2)}) collective-permute-start(bf16[8,128,512]{2,1,0:T(8,128)(2,1)S(1)} %collective-permute-done.3), channel_id=1, source_target_pairs={{0,4},{4,8},{8,12},{12,16},{16,20},{20,24},{24,28},{28,0},{1,5},{5... | collective-permute-start | bytes 3145736 | tf_op jit(solution)/shard_map/ppermute | solution.py:51
  60.7 23.4 %collective-permute-start.4 = (bf16[8,128,512]{2,1,0:T(8,128)(2,1)S(1)}, bf16[8,128,512]{2,1,0:T(8,128)(2,1)S(1)}, u32[]{:S(2)}, u32[]{:S(2)}) collective-permute-start(bf16[8,128,512]{2,1,0:T(8,128)(2,1)S(1)} %collective-permute-done.2), channel_id=1, source_target_pairs={{0,28},{4,0},{8,4},{12,8},{16,12},{20,16},{24,20},{28,24},{1,29},{... | collective-permute-start | bytes 3145736 | tf_op jit(solution)/shard_map/ppermute | solution.py:53
  71.9 19.4 %collective-permute-start.6 = (bf16[8,128,512]{2,1,0:T(8,128)(2,1)S(1)}, bf16[8,128,512]{2,1,0:T(8,128)(2,1)S(1)}, u32[]{:S(2)}, u32[]{:S(2)}) collective-permute-start(bf16[8,128,512]{2,1,0:T(8,128)(2,1)S(1)} %collective-permute-done.5), channel_id=1, source_target_pairs={{0,4},{4,8},{8,12},{12,16},{16,20},{20,24},{24,28},{28,0},{1,5},{5... | collective-permute-start | bytes 3145736 | tf_op jit(solution)/shard_map/ppermute | solution.py:51
  117.7 0.7 copy-start.2
  269.4 30.3 %all-to-all-start = ((bf16[8,256,512]{1,2,0:T(8,128)(2,1)}), bf16[8,256,512]{1,2,0:T(8,128)(2,1)S(1)}, u32[]{:S(2)}, u32[]{:S(2)}) async-start(bf16[8,256,512]{1,2,0:T(8,128)(2,1)} %select_select_fusion), calls=%async_computation.1 | async-start | bytes 4194304 | tf_op jit(solution)/shard_map/all_to_all | solution.py:78
Sparse Core Ops, SparseCore 0:
  117.8 147.4 reduce-scatter.1
